TPU v7x, 32 devices: a whole 2x2x4 slice. The times are simulated.
32 devices in a mesh: cp: 32 (over z, y, x, core).
Axes of the slice: x: 2, y: 2, z: 4, core: 2. Of those that a mesh axis runs over, the one named last changes fastest.
Arguments:
- queries: bfloat16 [16384, 512], P('cp'), may hold values from -6 to 6
- keys: bfloat16 [16384, 128], P('cp'), may hold values from -6 to 6
- values: bfloat16 [16384, 128], P('cp'), may hold values from -6 to 6
- grad_out: bfloat16 [16384, 512], P('cp'), may hold values from -6 to 6
- selections: int32 [32, 2], P('cp'), may hold values from -1 to 30, as said below
Outputs:
- attended: bfloat16 [16384, 512], P('cp')
- grad_queries: bfloat16 [16384, 512], P('cp')
- grad_keys: bfloat16 [16384, 128], P('cp')
- grad_values: bfloat16 [16384, 128], P('cp')
Inputs may be any that keep to these rules, and one draw needn't show every extreme that they name: `selections`: row b names two different blocks before block b; where block b has fewer than two earlier blocks, the missing entries are -1 (blocks 0 and 1 only).
All inputs are finite; a program needn't handle non-finite values.
Results may differ from a plain program's by a relative error of at most 0.015.
Values may be sent and summed in bfloat16 or wider, within the bound.
No kernel may reach another device: no remote copies, remote signals or barrier semaphores. Data moves between devices by JAX's collectives and lax.ppermute only.
A program may use at most 128 MiB of HBM per device.

v0:
```python
import jax
import jax.numpy as jnp
from jax import lax
from jax.sharding import PartitionSpec as P

HEADS = 4
HEAD_DIM = 128
BLK = 512


masked_value = -1e30


def key_mask(chosen):
    rows_at = lax.broadcasted_iota(jnp.int32, (BLK, BLK), 0)
    cols_at = lax.broadcasted_iota(jnp.int32, (BLK, BLK), 1)
    causal = cols_at <= rows_at
    first_ok = jnp.broadcast_to(chosen[0] >= 0, (BLK, BLK))
    second_ok = jnp.broadcast_to(chosen[1] >= 0, (BLK, BLK))
    return jnp.concatenate([causal, first_ok, second_ok], axis=1)


def attend_forward(query_rows, block_keys, allowed):
    score_scale = HEAD_DIM ** (-0.5)
    query_heads = query_rows.reshape(BLK, HEADS, HEAD_DIM)
    scores = (
        jnp.einsum("qhd,kd->hqk", query_heads, block_keys, preferred_element_type=jnp.float32)
        * score_scale
    )
    scores = jnp.where(allowed[None], scores, masked_value)
    row_max = jnp.max(scores, axis=-1, keepdims=True)
    exponent = jnp.exp(scores - row_max)
    weights = exponent / jnp.sum(exponent, axis=-1, keepdims=True)
    return (query_heads, weights, weights.astype(jnp.bfloat16))


def body(queries, keys, values, grad_out, selections):
    devices = lax.axis_size("cp")
    local_rows = queries.shape[0]
    local_blocks = local_rows // BLK
    piece_rows = BLK // devices
    head_width = keys.shape[1]
    pair_width = 2 * head_width
    score_scale = HEAD_DIM ** (-0.5)
    requests = lax.all_gather(selections, "cp", axis=0, tiled=True)
    local_pairs = jnp.concatenate([keys, values], axis=1)

    def block_inputs(member, gathered):
        joined = jnp.concatenate(
            [local_pairs, gathered[2 * member], gathered[2 * member + 1]], axis=0
        )
        return (joined[:, :head_width], joined[:, head_width:], key_mask(selections[member]))

    spread = lax.all_to_all(
        local_pairs.reshape(local_blocks, devices, piece_rows, pair_width),
        "cp",
        split_axis=1,
        concat_axis=0,
        tiled=True,
    )
    held_pieces = spread.reshape(local_blocks * devices, piece_rows, pair_width)
    wanted = jnp.maximum(requests, 0)
    outgoing = held_pieces[wanted]
    arrived = lax.all_to_all(outgoing, "cp", split_axis=0, concat_axis=2, tiled=True)
    fetched = arrived.reshape(2 * local_blocks, BLK, pair_width)
    member = 0
    block_keys, block_values, allowed = block_inputs(member, fetched)
    query_heads, weights, probs_low = attend_forward(queries, block_keys, allowed)
    output_heads = jnp.einsum(
        "hqk,kd->qhd", probs_low, block_values, preferred_element_type=jnp.float32
    )
    attended = output_heads.astype(jnp.bfloat16).reshape(BLK, HEADS * HEAD_DIM)
    slot_grads = []
    member = 0
    block_keys, block_values, allowed = block_inputs(member, fetched)
    query_heads, weights, probs_low = attend_forward(queries, block_keys, allowed)
    grad_heads = grad_out.reshape(BLK, HEADS, HEAD_DIM)
    grad_probs = jnp.einsum(
        "qhd,kd->hqk", grad_heads, block_values, preferred_element_type=jnp.float32
    )
    inner_sum = jnp.sum(weights * grad_probs, axis=-1, keepdims=True)
    grad_scores = (weights * (grad_probs - inner_sum)).astype(jnp.bfloat16)
    grad_query = (
        jnp.einsum("hqk,kd->qhd", grad_scores, block_keys, preferred_element_type=jnp.float32)
        * score_scale
    )
    grad_queries = grad_query.astype(jnp.bfloat16).reshape(BLK, HEADS * HEAD_DIM)
    grad_k = (
        jnp.einsum("hqk,qhd->kd", grad_scores, query_heads, preferred_element_type=jnp.float32)
        * score_scale
    )
    grad_v = jnp.einsum("hqk,qhd->kd", probs_low, grad_heads, preferred_element_type=jnp.float32)
    grad_both = jnp.concatenate([grad_k, grad_v], axis=1)
    own_grads = grad_both[:BLK]
    slot_grads.append(grad_both[BLK : 2 * BLK])
    slot_grads.append(grad_both[2 * BLK :])
    partials = jnp.stack(slot_grads).reshape(2 * local_blocks, devices, piece_rows, pair_width)
    received = lax.all_to_all(
        partials.astype(jnp.bfloat16), "cp", split_axis=1, concat_axis=1, tiled=True
    ).astype(partials.dtype)
    owners_ids = requests.T.reshape(-1)
    total_blocks = devices * local_blocks
    onehot = (owners_ids[None, :] == jnp.arange(total_blocks, dtype=jnp.int32)[:, None]).astype(
        jnp.float32
    )
    summed = jnp.dot(
        onehot,
        received.reshape(2 * local_blocks * devices, piece_rows * pair_width),
        precision=lax.Precision.HIGHEST,
    )
    returned = lax.all_to_all(
        summed.reshape(devices, local_blocks, piece_rows, pair_width).astype(jnp.bfloat16),
        "cp",
        split_axis=0,
        concat_axis=2,
        tiled=True,
    ).astype(jnp.float32)
    grad_pairs = returned.reshape(local_rows, pair_width) + own_grads
    return (
        attended,
        grad_queries,
        grad_pairs[:, :head_width].astype(jnp.bfloat16),
        grad_pairs[:, head_width:].astype(jnp.bfloat16),
    )


def solution(mesh):
    in_specs = (P("cp", None), P("cp", None), P("cp", None), P("cp", None), P("cp", None))
    out_specs = (P("cp", None), P("cp", None), P("cp", None), P("cp", None))
    return jax.shard_map(body, mesh=mesh, in_specs=in_specs, out_specs=out_specs, check_vma=False)
```

profile of v0, /device:TPU:0, one launch (start us, length us, event | category | flops | bytes accessed | tf_op | source)
XLA Modules:
  0.0 151.7 jit_solution(15815537463073276769)
XLA Ops:
  0.6 1.6 %constant_dynamic-update-slice_fusion.1 = bf16[512,256]{1,0:T(8,128)(2,1)} fusion(bf16[512,128]{1,0:T(8,128)(2,1)} %param.6), kind=kLoop, calls=%fused_computation.49 | loop fusion | bytes 262144
  2.2 1.6 %constant_dynamic-update-slice_fusion = bf16[512,256]{1,0:T(8,128)(2,1)} fusion(bf16[512,256]{1,0:T(8,128)(2,1)} %constant_dynamic-update-slice_fusion.1, bf16[512,128]{1,0:T(8,128)(2,1)} %param.7), kind=kLoop, calls=%fused_computation.48 | loop fusion | bytes 262144 | tf_op jit(solution)/shard_map/concatenate | solution.py:46
  3.8 7.3 %all-to-all-start = ((bf16[1,32,16,256]{3,2,0,1:T(8,128)(2,1)}), bf16[1,32,16,256]{3,2,0,1:T(8,128)(2,1)S(1)}, u32[]{:S(2)}, u32[]{:S(2)}) async-start(bf16[1,32,16,256]{3,2,0,1:T(8,128)(2,1)} %bitcast.1), calls=%async_computation | async-start | bytes 524288 | tf_op jit(solution)/shard_map/all_to_all | solution.py:54
  11.1 42.0 %all-gather = s32[32,1,2]{2,1,0:T(1,128)S(1)} all-gather(s32[1,1,2]{2,1,0:T(1,128)} %bitcast.108), channel_id=1, replica_groups=mesh['cp'=32] {'cp'}, dimensions={0}, use_global_device_ids=true | all-gather | bytes 264 | tf_op jit(solution)/shard_map/all_gather | solution.py:45
  53.4 1.4 gather_fusion
  54.8 2.6 %all-to-all-start.1 = ((bf16[32,2,16,256]{3,2,1,0:T(8,128)(2,1)}), bf16[32,2,16,256]{3,2,1,0:T(8,128)(2,1)S(1)}, u32[]{:S(2)}, u32[]{:S(2)}) async-start(bf16[32,2,16,256]{3,2,1,0:T(8,128)(2,1)} %bitcast.5), calls=%async_computation.1 | async-start | bytes 1048576 | tf_op jit(solution)/shard_map/all_to_all | solution.py:64
  57.4 1.3 copy.80
  58.6 1.3 fusion.37
  61.3 1.3 copy.81
  62.7 2.2 %add_add_fusion = pred[512,1536]{0,1:T(8,128)(4,1)} fusion(pred[512,512]{0,1:T(8,128)(4,1)S(1)} %iota_compare_fusion, pred[1536]{0:T(1024)(128)(4,1)S(1)} %pad.6.clone, pred[1536]{0:T(1024)(128)(4,1)S(1)} %pad.5.clone), kind=kLoop, calls=%fused_computation.18 | loop fusion | flops 1572864 | bytes 1051648 | tf_op jit(solution)/shard_map/concatenate | solution.py:20
  64.9 8.1 %all-to-all-done.1 = bf16[32,2,16,256]{3,2,1,0:T(8,128)(2,1)S(1)} async-done(((bf16[32,2,16,256]{3,2,1,0:T(8,128)(2,1)}), bf16[32,2,16,256]{3,2,1,0:T(8,128)(2,1)S(1)}, u32[]{:S(2)}, u32[]{:S(2)}) %all-to-all-start.1) | async-done | bytes 524320 | tf_op jit(solution)/shard_map/all_to_all | solution.py:64
  73.0 1.0 pad_maximum_fusion.1
  74.0 6.3 %fusion.28 = f32[1536,512,4]{1,0,2:T(8,128)} fusion(bf16[512,4,128]{0,2,1:T(8,128)(2,1)S(1)} %bitcast.96, bf16[1536,256]{1,0:T(8,128)(2,1)S(1)} %pad_maximum_fusion.1), kind=kOutput, calls=%fused_computation.42 | convolution fusion | flops 805306368 | bytes 13500416 | tf_op jit(solution)/shard_map/qhd,kd->hqk/dot_general | solution.py:27
  80.3 11.7 %fusion.38 = (f32[4,512]{1,0:T(4,128)S(1)}, f32[4,512,1536]{1,2,0:T(8,128)S(1)}) fusion(f32[1536,512,4]{1,0,2:T(8,128)} %fusion.28, pred[512,1536]{0,1:T(8,128)(4,1)} %add_add_fusion), kind=kOutput, calls=%fused_computation.57 | output fusion | flops 18875904 | bytes 25960448 | tf_op jit(solution)/shard_map/sub | solution.py:32
  92.0 5.9 %fusion.1 = (f32[4,512]{1,0:T(4,128)S(1)}, f32[1536,512,4]{1,0,2:T(8,128)}) fusion(f32[4,512,1536]{1,2,0:T(8,128)S(1)} %get-tuple-element.25, f32[4,512]{1,0:T(4,128)S(1)} %get-tuple-element.24, bf16[512,4,128]{0,2,1:T(8,128)(2,1)S(1)} %bitcast.105, bf16[1536,256]{1,0:T(8,128)(2,1)S(1)} %pad_maximum_fusion.1), kind=kOutput, calls=%fused_computation.4 | convolution fusion | flops 814741504 | bytes 26099712 | tf_op jit(solution)/shard_map/qhd,kd->hqk/dot_general | solution.py:78
  98.0 2.2 %fusion.12 = f32[1536,128]{0,1:T(8,128)S(1)} fusion(bf16[512,4,128]{0,2,1:T(8,128)(2,1)S(1)} %bitcast.106, f32[4,512,1536]{1,2,0:T(8,128)S(1)} %get-tuple-element.25, f32[4,512]{1,0:T(4,128)S(1)} %get-tuple-element.24), kind=kOutput, calls=%fused_computation.19 | convolution fusion | flops 811597824 | bytes 13901824 | tf_op jit(solution)/shard_map/hqk,qhd->kd/dot_general | solution.py:92
  100.3 6.8 %fusion.3 = bf16[4,512,1536]{1,2,0:T(8,128)(2,1)S(1)} fusion(f32[1536,512,4]{1,0,2:T(8,128)} %get-tuple-element.27, f32[4,512]{1,0:T(4,128)S(1)} %get-tuple-element.26, f32[4,512,1536]{1,2,0:T(8,128)S(1)} %get-tuple-element.25, f32[4,512]{1,0:T(4,128)S(1)} %get-tuple-element.24), kind=kLoop, calls=%fused_computation.6 | loop fusion | flops 12582912 | bytes 31473664 | tf_op jit(solution)/shard_map/convert_element_type | solution.py:82
  107.2 2.6 %copy-done = bf16[4,512,1536]{1,2,0:T(8,128)(2,1)} copy-done((bf16[4,512,1536]{1,2,0:T(8,128)(2,1)}, bf16[4,512,1536]{1,2,0:T(8,128)(2,1)S(1)}, u32[]{:S(2)}) %copy-start) | copy-done | bytes 6291480
  109.7 2.1 %fusion.15 = f32[1536,128]{0,1:T(8,128)S(1)} fusion(bf16[4,512,1536]{1,2,0:T(8,128)(2,1)S(1)} %fusion.3, bf16[512,4,128]{0,2,1:T(8,128)(2,1)S(1)} %bitcast.97), kind=kOutput, calls=%fused_computation.21 | convolution fusion | flops 805502976 | bytes 7602176 | tf_op jit(solution)/shard_map/hqk,qhd->kd/dot_general | solution.py:89
  112.0 0.8 copy-done.3
  113.2 0.9 copy.62
  114.0 2.9 %all-to-all-start.2 = ((bf16[2,32,16,256]{3,2,0,1:T(8,128)(2,1)}), bf16[2,32,16,256]{3,2,0,1:T(8,128)(2,1)S(1)}, u32[]{:S(2)}, u32[]{:S(2)}) async-start(bf16[2,32,16,256]{3,2,0,1:T(8,128)(2,1)} %copy.62), calls=%async_computation.2 | async-start | bytes 1048576 | tf_op jit(solution)/shard_map/all_to_all | solution.py:98
  117.0 15.5 %all-to-all-done.2 = bf16[2,32,16,256]{3,2,0,1:T(8,128)(2,1)S(1)} async-done(((bf16[2,32,16,256]{3,2,0,1:T(8,128)(2,1)}), bf16[2,32,16,256]{3,2,0,1:T(8,128)(2,1)S(1)}, u32[]{:S(2)}, u32[]{:S(2)}) %all-to-all-start.2) | async-done | bytes 524320 | tf_op jit(solution)/shard_map/all_to_all | solution.py:98
  132.8 0.9 copy.65
  133.7 3.5 %all-to-all-start.3 = ((bf16[32,1,16,256]{3,2,1,0:T(8,128)(2,1)}), bf16[32,1,16,256]{3,2,1,0:T(8,128)(2,1)}, u32[]{:S(2)}, u32[]{:S(2)}) async-start(bf16[32,1,16,256]{3,2,1,0:T(8,128)(2,1)} %copy.65), calls=%async_computation.3 | async-start | bytes 524288 | tf_op jit(solution)/shard_map/all_to_all | solution.py:111
  137.2 6.5 %fusion.18 = bf16[128,4,512]{2,0,1:T(8,128)(2,1)} fusion(bf16[1536,256]{1,0:T(8,128)(2,1)S(1)} %pad_maximum_fusion.1, f32[4,512,1536]{1,2,0:T(8,128)} %copy-done.1, f32[4,512]{1,0:T(4,128)S(1)} %get-tuple-element.24), kind=kOutput, calls=%fused_computation.28 | convolution fusion | flops 811859968 | bytes 13508608 | tf_op jit(solution)/shard_map/hqk,kd->qhd/dot_general | solution.py:69
  143.7 1.0 fusion.17
  144.8 1.0 copy.69
  145.8 2.0 %copy.68 = bf16[512,512]{1,0:T(8,128)(2,1)} copy(bf16[512,512]{0,1:T(8,128)(2,1)} %bitcast.107) | data formatting | bytes 1048576
  147.8 1.0 bitcast_convert_fusion
  149.0 1.1 fusion.24
  150.1 0.8 copy.70
  (35 shorter events, 2.4 us)
Async XLA Ops:
  3.8 49.6 %all-to-all-start = ((bf16[1,32,16,256]{3,2,0,1:T(8,128)(2,1)}), bf16[1,32,16,256]{3,2,0,1:T(8,128)(2,1)S(1)}, u32[]{:S(2)}, u32[]{:S(2)}) async-start(bf16[1,32,16,256]{3,2,0,1:T(8,128)(2,1)} %bitcast.1), calls=%async_computation | async-start | bytes 524288 | tf_op jit(solution)/shard_map/all_to_all | solution.py:54
  54.8 18.2 %all-to-all-start.1 = ((bf16[32,2,16,256]{3,2,1,0:T(8,128)(2,1)}), bf16[32,2,16,256]{3,2,1,0:T(8,128)(2,1)S(1)}, u32[]{:S(2)}, u32[]{:S(2)}) async-start(bf16[32,2,16,256]{3,2,1,0:T(8,128)(2,1)} %bitcast.5), calls=%async_computation.1 | async-start | bytes 1048576 | tf_op jit(solution)/shard_map/all_to_all | solution.py:64
  92.0 8.3 %copy-start.1 = (f32[4,512,1536]{1,2,0:T(8,128)}, f32[4,512,1536]{1,2,0:T(8,128)S(1)}, u32[]{:S(2)}) copy-start(f32[4,512,1536]{1,2,0:T(8,128)S(1)} %get-tuple-element.25) | copy-start | bytes 37748740
  100.2 11.7 %copy-start.2 = (f32[1536,128]{0,1:T(8,128)}, f32[1536,128]{0,1:T(8,128)S(1)}, u32[]{:S(2)}) copy-start(f32[1536,128]{0,1:T(8,128)S(1)} %fusion.12) | copy-start | bytes 2359300
  107.2 2.6 %copy-start = (bf16[4,512,1536]{1,2,0:T(8,128)(2,1)}, bf16[4,512,1536]{1,2,0:T(8,128)(2,1)S(1)}, u32[]{:S(2)}) copy-start(bf16[4,512,1536]{1,2,0:T(8,128)(2,1)S(1)} %fusion.3) | copy-start | bytes 18874372
  111.9 0.9 copy-start.3
  114.0 18.5 %all-to-all-start.2 = ((bf16[2,32,16,256]{3,2,0,1:T(8,128)(2,1)}), bf16[2,32,16,256]{3,2,0,1:T(8,128)(2,1)S(1)}, u32[]{:S(2)}, u32[]{:S(2)}) async-start(bf16[2,32,16,256]{3,2,0,1:T(8,128)(2,1)} %copy.62), calls=%async_computation.2 | async-start | bytes 1048576 | tf_op jit(solution)/shard_map/all_to_all | solution.py:98
  132.8 10.9 %slice-start = ((s8[6291456]{0:T(1024)(128)(4,1)}), s8[2097152]{0:T(1024)(128)(4,1)S(1)}, s32[]{:S(2)}) async-start(s8[6291456]{0:T(1024)(128)(4,1)} %bitcast.93), calls=%async_computation.4 | async-start | bytes 4194304
  133.7 14.1 %all-to-all-start.3 = ((bf16[32,1,16,256]{3,2,1,0:T(8,128)(2,1)}), bf16[32,1,16,256]{3,2,1,0:T(8,128)(2,1)}, u32[]{:S(2)}, u32[]{:S(2)}) async-start(bf16[32,1,16,256]{3,2,1,0:T(8,128)(2,1)} %copy.65), calls=%async_computation.3 | async-start | bytes 524288 | tf_op jit(solution)/shard_map/all_to_all | solution.py:111
  137.2 6.5 %slice-start.1 = ((s8[6291456]{0:T(1024)(128)(4,1)}), s8[4194304]{0:T(1024)(128)(4,1)S(1)}, s32[]{:S(2)}) async-start(s8[6291456]{0:T(1024)(128)(4,1)} %bitcast.93), calls=%async_computation.5 | async-start | bytes 8388608
where the time goes:
time: 152 us
  blocking collectives  42 us (28%)
  matrix products  24.4 us (16%)
  other arithmetic  24 us (16%)
  waiting for transfers between devices  23.6 us (16%)
  local copies, waits for them, and re-layouts  19.1 us (13%)
  starting transfers between devices  16.3 us (11%)
  between operations  2.2 us (1%)
    all_gather x1, blocking collectives, body(): requests = lax.all_gather(selections, 'cp', axis=0, tiled=True)  42 us
    all_to_all x1, waiting for transfers between devices, body(): lax.all_to_all(partials.astype(jnp.bfloat16), 'cp', split_axis=1, concat_...  15.5 us
    sub x1, other arithmetic, attend_forward(): exponent = jnp.exp(scores - row_max)  11.7 us
    unnamed x17, local copies, waits for them, and re-layouts  9.67 us
    all_to_all x1, waiting for transfers between devices, body(): lax.all_to_all(outgoing, 'cp', split_axis=0, concat_axis=2, tiled=True)  8.1 us
    all_to_all x1, starting transfers between devices, body(): lax.all_to_all(local_pairs.reshape(local_blocks, devices, piece_rows, pai...  7.33 us
    convert_element_type x1, other arithmetic, body(): grad_scores = (weights * (grad_probs - inner_sum)).astype(jnp.bfloat16)  6.82 us
    dot_general x1, matrix products, body(): jnp.einsum('hqk,kd->qhd', probs_low, block_values, preferred_element_type...  6.53 us
  transfers between devices with their start and end apart: 4, of which 2 were waited for; matrix products, arithmetic and copies ran while one was open for 11% of the time, Pallas kernels for 0%

commit v1 on v0

v1 whole, which is shorter than its diff:
```python
import functools

import jax
import jax.numpy as jnp
from jax import lax
from jax.experimental import pallas as pl
from jax.experimental.pallas import tpu as pltpu
from jax.sharding import PartitionSpec as P

HEADS = 4
HEAD_DIM = 128
BLK = 512
SUB = 8
DIGIT = 128
SCALE = HEAD_DIM ** (-0.5)
LOG2_SCALE = SCALE * 1.4426950408889634
MASKED = -1e30

f32 = jnp.float32
bf16 = jnp.bfloat16


def dot(a, b):
    return lax.dot_general(a, b, (((1,), (0,)), ((), ())), preferred_element_type=f32)


def vmem():
    return pl.BlockSpec(memory_space=pltpu.VMEM)


def smem():
    return pl.BlockSpec(memory_space=pltpu.SMEM)


def params(mib=40):
    return pltpu.CompilerParams(vmem_limit_bytes=mib * 1024 * 1024)


def cost(flops, trans=0, nbytes=1024):
    return pl.CostEstimate(flops=flops, transcendentals=trans, bytes_accessed=nbytes)


def pack_kernel(sel_ref, keys_ref, values_ref, out_ref):
    parts, rows, width = out_ref.shape
    rows = rows - SUB
    half = parts // 2
    out_ref[:half, :rows, :] = keys_ref[...].reshape(half, rows, width)
    out_ref[half:, :rows, :] = values_ref[...].reshape(half, rows, width)
    lane = lax.broadcasted_iota(jnp.int32, (SUB, width), 1)
    ids = jnp.zeros((SUB, width), jnp.int32)
    for slot in range(2):
        number = sel_ref[0, slot] + 1
        ids = jnp.where(lane == 2 * slot, lax.shift_right_logical(number, 7), ids)
        ids = jnp.where(lane == 2 * slot + 1, number & (DIGIT - 1), ids)
    tail = ids.astype(f32).astype(bf16)
    out_ref[:, rows:, :] = jnp.broadcast_to(tail[None], (parts, SUB, width))


def request_of(ids_ref, reader, slot):
    return ids_ref[reader, 2 * slot] * DIGIT + ids_ref[reader, 2 * slot + 1] - 1


def gather_kernel(held_ref, out_ref, ids_ref, ids_smem, sem):
    readers, _, rows, width = out_ref.shape
    tail = held_ref[:, rows:, :].astype(f32)
    ids_ref[...] = jnp.max(tail, axis=1).astype(jnp.int32)
    copy = pltpu.make_async_copy(ids_ref, ids_smem, sem)
    copy.start()
    copy.wait()

    def one(reader, carry):
        for slot in range(2):
            block = jnp.maximum(request_of(ids_smem, reader, slot), 0)
            out_ref[reader, slot] = held_ref[block, :rows, :]
        return carry

    lax.fori_loop(0, readers, one, 0, unroll=8)


def pre_kernel(queries_ref, grad_ref, keys_ref, values_ref, qt_ref, gt_ref, stats_ref):
    keys = keys_ref[...]
    values = values_ref[...]
    key_at = lax.broadcasted_iota(jnp.int32, (BLK, BLK), 0)
    query_at = lax.broadcasted_iota(jnp.int32, (BLK, BLK), 1)
    causal = key_at <= query_at
    for h in range(HEADS):
        cols = slice(h * HEAD_DIM, (h + 1) * HEAD_DIM)
        qt = queries_ref[:, cols].T
        gt = grad_ref[:, cols].T
        qt_ref[h] = qt
        gt_ref[h] = gt
        scores = jnp.where(causal, dot(keys, qt), MASKED)
        top = jnp.max(scores, axis=0, keepdims=True)
        weight = jnp.exp2(scores * LOG2_SCALE - top * LOG2_SCALE)
        stats_ref[h, 0:1, :] = top
        stats_ref[h, 1:2, :] = jnp.sum(weight, axis=0, keepdims=True)
        stats_ref[h, 2:3, :] = jnp.sum(weight * dot(values, gt), axis=0, keepdims=True)


def slot_terms(sel_ref, slot):
    ok = sel_ref[0, slot] >= 0
    return jnp.where(ok, 1.0, 0.0), jnp.where(ok, 0.0, 1e30), jnp.where(ok, 0.0, MASKED)


def main_kernel(sel_ref, fetched_ref, qt_ref, gt_ref, queries_ref, grad_ref, own_ref, out_ref, stats_ref):
    parts, _, rows, width = fetched_ref.shape
    half = parts // 2
    keys = [fetched_ref[:half, s].reshape(BLK, width) for s in range(2)]
    values = [fetched_ref[half:, s].reshape(BLK, width) for s in range(2)]
    terms = [slot_terms(sel_ref, s) for s in range(2)]
    grad_k = [None, None]
    grad_v = [None, None]
    for h in range(HEADS):
        cols = slice(h * HEAD_DIM, (h + 1) * HEAD_DIM)
        qt = qt_ref[h]
        gt = gt_ref[h]
        q_h = queries_ref[:, cols]
        g_h = grad_ref[:, cols]
        top0 = own_ref[h, 0:1, :]
        scores = [dot(keys[s], qt) for s in range(2)]
        top = top0
        for s in range(2):
            _, _, low = terms[s]
            keep, _, _ = terms[s]
            top = jnp.maximum(top, jnp.max(scores[s], axis=0, keepdims=True) * keep + low)
        base = top * LOG2_SCALE
        alpha = jnp.exp2(top0 * LOG2_SCALE - base)
        total = own_ref[h, 1:2, :] * alpha
        inner = own_ref[h, 2:3, :] * alpha
        weight = []
        for s in range(2):
            keep, high, _ = terms[s]
            w = jnp.exp2(scores[s] * (keep * LOG2_SCALE) - (base * keep + high))
            weight.append(w)
            total = total + jnp.sum(w, axis=0, keepdims=True)
        inverse = 1.0 / total
        inner = inner * inverse
        grads = []
        for s in range(2):
            weight[s] = weight[s] * inverse
            grads.append(dot(values[s], gt))
            inner = inner + jnp.sum(weight[s] * grads[s], axis=0, keepdims=True)
        for s in range(2):
            dv = dot(weight[s].astype(bf16), g_h)
            grad_v[s] = dv if grad_v[s] is None else grad_v[s] + dv
            ds = (weight[s] * (grads[s] - inner)).astype(bf16)
            dk = dot(ds, q_h)
            grad_k[s] = dk if grad_k[s] is None else grad_k[s] + dk
        stats_ref[h, 0:1, :] = base
        stats_ref[h, 1:2, :] = inverse
        stats_ref[h, 2:3, :] = inner
    for s in range(2):
        out_ref[:half, s] = (grad_k[s] * SCALE).astype(bf16).reshape(half, rows, width)
        out_ref[half:, s] = grad_v[s].astype(bf16).reshape(half, rows, width)


def selected_kernel(sel_ref, fetched_ref, qt_ref, gt_ref, stats_ref, att_ref, dq_ref):
    parts, _, rows, width = fetched_ref.shape
    half = parts // 2
    terms = [slot_terms(sel_ref, s) for s in range(2)]
    keys = [fetched_ref[:half, s].reshape(BLK, width) for s in range(2)]
    values = [fetched_ref[half:, s].reshape(BLK, width) for s in range(2)]
    keys_t = [k.T for k in keys]
    values_t = [v.T for v in values]
    for h in range(HEADS):
        base = stats_ref[h, 0:1, :]
        inverse = stats_ref[h, 1:2, :]
        inner = stats_ref[h, 2:3, :]
        att = None
        dq = None
        for s in range(2):
            keep, high, _ = terms[s]
            scores = dot(keys[s], qt_ref[h])
            w = jnp.exp2(scores * (keep * LOG2_SCALE) - (base * keep + high)) * inverse
            ds = (w * (dot(values[s], gt_ref[h]) - inner)).astype(bf16)
            att_s = dot(values_t[s], w.astype(bf16))
            dq_s = dot(keys_t[s], ds)
            att = att_s if att is None else att + att_s
            dq = dq_s if dq is None else dq + dq_s
        att_ref[h] = att
        dq_ref[h] = dq


def own_kernel(keys_ref, values_ref, qt_ref, gt_ref, queries_ref, grad_ref, stats_ref, att_ref, dq_ref, att_out, dq_out, own_out):
    keys = keys_ref[...]
    values = values_ref[...]
    keys_t = keys.T
    values_t = values.T
    key_at = lax.broadcasted_iota(jnp.int32, (BLK, BLK), 0)
    query_at = lax.broadcasted_iota(jnp.int32, (BLK, BLK), 1)
    causal = key_at <= query_at
    grad_k = None
    grad_v = None
    for h in range(HEADS):
        cols = slice(h * HEAD_DIM, (h + 1) * HEAD_DIM)
        base = stats_ref[h, 0:1, :]
        inverse = stats_ref[h, 1:2, :]
        inner = stats_ref[h, 2:3, :]
        scores = jnp.where(causal, dot(keys, qt_ref[h]) * LOG2_SCALE, MASKED)
        w = jnp.exp2(scores - base) * inverse
        low = w.astype(bf16)
        ds = (w * (dot(values, gt_ref[h]) - inner)).astype(bf16)
        att = att_ref[h] + dot(values_t, low)
        dq = (dq_ref[h] + dot(keys_t, ds)) * SCALE
        att_out[:, cols] = att.T.astype(bf16)
        dq_out[:, cols] = dq.T.astype(bf16)
        dv = dot(low, grad_ref[:, cols])
        dk = dot(ds, queries_ref[:, cols])
        grad_v = dv if grad_v is None else grad_v + dv
        grad_k = dk if grad_k is None else grad_k + dk
    own_out[:BLK, :] = grad_k * SCALE
    own_out[BLK:, :] = grad_v


def sum_kernel(ids_ref, received_ref, out_ref, acc_ref):
    readers = received_ref.shape[0]
    acc_ref[...] = jnp.zeros(acc_ref.shape, f32)

    def one(reader, carry):
        for slot in range(2):
            block = jnp.maximum(request_of(ids_ref, reader, slot), 0)
            acc_ref[block] = acc_ref[block] + received_ref[reader, slot].astype(f32)
        return carry

    lax.fori_loop(0, readers, one, 0, unroll=8)
    out_ref[...] = acc_ref[...].astype(bf16)


def final_kernel(returned_ref, own_ref, dk_ref, dv_ref):
    parts, rows, width = returned_ref.shape
    half = parts // 2
    dk_ref[...] = (returned_ref[:half].reshape(BLK, width).astype(f32) + own_ref[:BLK, :]).astype(bf16)
    dv_ref[...] = (returned_ref[half:].reshape(BLK, width).astype(f32) + own_ref[BLK:, :]).astype(bf16)


def exchange(array):
    return lax.all_to_all(array, "cp", split_axis=0, concat_axis=0, tiled=True)


def body(queries, keys, values, grad_out, selections):
    parts = lax.axis_size("cp")
    width = keys.shape[1]
    rows = 2 * BLK // parts
    shape = jax.ShapeDtypeStruct
    unit = 2 * HEADS * BLK * BLK * HEAD_DIM

    packed = pl.pallas_call(
        pack_kernel,
        out_shape=shape((parts, rows + SUB, width), bf16),
        in_specs=[smem(), vmem(), vmem()],
        out_specs=vmem(),
        compiler_params=params(),
        cost_estimate=cost(1000000),
        name="pack",
    )(selections, keys, values)
    held = exchange(packed)
    heads_t = shape((HEADS, HEAD_DIM, BLK), bf16)
    stats = shape((HEADS, SUB, BLK), f32)
    q_t, g_t, own_stats = pl.pallas_call(
        pre_kernel,
        out_shape=(heads_t, heads_t, stats),
        in_specs=[vmem()] * 4,
        out_specs=(vmem(),) * 3,
        compiler_params=params(),
        cost_estimate=cost(2 * unit, HEADS * BLK * BLK),
        name="pre",
    )(queries, grad_out, keys, values)
    outgoing, ids = pl.pallas_call(
        gather_kernel,
        out_shape=(shape((parts, 2, rows, width), bf16), shape((parts, width), jnp.int32)),
        in_specs=[vmem()],
        out_specs=(vmem(), vmem()),
        scratch_shapes=[pltpu.SMEM((parts, width), jnp.int32), pltpu.SemaphoreType.DMA],
        compiler_params=params(),
        cost_estimate=cost(1000000),
        name="gather",
    )(held)
    fetched = exchange(outgoing)
    partial, full_stats = pl.pallas_call(
        main_kernel,
        out_shape=(shape((parts, 2, rows, width), bf16), stats),
        in_specs=[smem()] + [vmem()] * 6,
        out_specs=(vmem(), vmem()),
        compiler_params=params(56),
        cost_estimate=cost(8 * unit, 2 * HEADS * BLK * BLK),
        name="main",
    )(selections, fetched, q_t, g_t, queries, grad_out, own_stats)
    received = exchange(partial)
    acc_t = shape((HEADS, HEAD_DIM, BLK), f32)
    att_t, dq_t = pl.pallas_call(
        selected_kernel,
        out_shape=(acc_t, acc_t),
        in_specs=[smem()] + [vmem()] * 4,
        out_specs=(vmem(), vmem()),
        compiler_params=params(56),
        cost_estimate=cost(8 * unit, 2 * HEADS * BLK * BLK),
        name="selected",
    )(selections, fetched, q_t, g_t, full_stats)
    summed = pl.pallas_call(
        sum_kernel,
        out_shape=shape((parts, rows, width), bf16),
        in_specs=[smem(), vmem()],
        out_specs=vmem(),
        scratch_shapes=[pltpu.VMEM((parts, rows, width), f32)],
        compiler_params=params(),
        cost_estimate=cost(1000000),
        name="sum",
    )(ids, received)
    returned = exchange(summed)
    attended, grad_queries, own_grads = pl.pallas_call(
        own_kernel,
        out_shape=(shape((BLK, HEADS * HEAD_DIM), bf16), shape((BLK, HEADS * HEAD_DIM), bf16), shape((2 * BLK, width), f32)),
        in_specs=[vmem()] * 9,
        out_specs=(vmem(),) * 3,
        compiler_params=params(56),
        cost_estimate=cost(6 * unit, HEADS * BLK * BLK),
        name="own",
    )(keys, values, q_t, g_t, queries, grad_out, full_stats, att_t, dq_t)
    grad_keys, grad_values = pl.pallas_call(
        final_kernel,
        out_shape=(shape((BLK, width), bf16), shape((BLK, width), bf16)),
        in_specs=[vmem(), vmem()],
        out_specs=(vmem(), vmem()),
        compiler_params=params(),
        cost_estimate=cost(1000000),
        name="final",
    )(returned, own_grads)
    return attended, grad_queries, grad_keys, grad_values


def solution(mesh):
    in_specs = (P("cp", None), P("cp", None), P("cp", None), P("cp", None), P("cp", None))
    out_specs = (P("cp", None), P("cp", None), P("cp", None), P("cp", None))
    return jax.shard_map(body, mesh=mesh, in_specs=in_specs, out_specs=out_specs, check_vma=False)
```

time: 152 us -> 92.8 us (0.61)
  Pallas kernels: 0 us -> 29.6 us
  matrix products: 24.4 us -> 0 us
  other arithmetic: 24 us -> 0 us
  local copies, waits for them, and re-layouts: 19.1 us -> 6.52 us
  waiting for transfers between devices: 23.6 us -> 11.9 us
  starting transfers between devices: 16.3 us -> 5.91 us
  blocking collectives: 42 us -> 37.7 us
    all_gather x1 -> x0, blocking collectives: 42 us -> none  [body(): requests = lax.all_gather(selections, 'cp', axis=0, tiled=True)]
    all_to_all x0 -> x2, blocking collectives: none -> 37.7 us  [exchange(): return lax.all_to_all(array, 'cp', split_axis=0, concat_axis=0, tiled=True)]
    pallas_call x0 -> x8, Pallas kernels: none -> 29.6 us  [the longest x1 10.1 us: body(): pl.pallas_call(main_kernel, out_shape=(shape((parts, 2, rows, width), bf1...]
    dot_general x7 -> x0, matrix products: 24.4 us -> none  [the longest x1 6.53 us: body(): jnp.einsum('hqk,kd->qhd', probs_low, block_values, preferred_element_type...]
    all_to_all x4 -> x2, waiting for transfers between devices: 23.6 us -> 11.9 us  [exchange(): return lax.all_to_all(array, 'cp', split_axis=0, concat_axis=0, tiled=True)]
    sub x1 -> x0, other arithmetic: 11.7 us -> none  [attend_forward(): exponent = jnp.exp(scores - row_max)]
    all_to_all x4 -> x2, starting transfers between devices: 16.3 us -> 5.91 us  [exchange(): return lax.all_to_all(array, 'cp', split_axis=0, concat_axis=0, tiled=True)]
    convert_element_type x2 -> x0, other arithmetic: 7.81 us -> none  [the longest x1 6.82 us: body(): grad_scores = (weights * (grad_probs - inner_sum)).astype(jnp.bfloat16)]
  transfers between devices with their start and end apart: 4 -> 2, of which waited for: 2 -> 1; matrix products, arithmetic and copies ran while one was open for 11% -> 0% of each run, Pallas kernels for 0% -> 16%
where the time goes in v1:
time: 92.8 us; the launch traced here: 92.3 us
  blocking collectives  37.7 us (41%)
  Pallas kernels  29.6 us (32%)
  waiting for transfers between devices  11.9 us (13%)
  local copies, waits for them, and re-layouts  6.52 us (7%)
  starting transfers between devices  5.91 us (6%)
    all_to_all x2, blocking collectives, exchange(): return lax.all_to_all(array, 'cp', split_axis=0, concat_axis=0, tiled=True)  37.7 us
    all_to_all x2, waiting for transfers between devices, exchange(): return lax.all_to_all(array, 'cp', split_axis=0, concat_axis=0, tiled=True)  11.9 us
    pallas_call x1, Pallas kernels, body(): pl.pallas_call(main_kernel, out_shape=(shape((parts, 2, rows, width), bf1...  10.1 us
    pallas_call x1, Pallas kernels, body(): pl.pallas_call(selected_kernel, out_shape=(acc_t, acc_t), in_specs=[smem(...  6.68 us
    unnamed x24, local copies, waits for them, and re-layouts  6.52 us
    pallas_call x1, Pallas kernels, body(): pl.pallas_call(own_kernel, out_shape=(shape((BLK, HEADS * HEAD_DIM), bf16...  6.35 us
    all_to_all x2, starting transfers between devices, exchange(): return lax.all_to_all(array, 'cp', split_axis=0, concat_axis=0, tiled=True)  5.91 us
    pallas_call x1, Pallas kernels, body(): pl.pallas_call(sum_kernel, out_shape=shape((parts, rows, width), bf16), i...  1.89 us
  transfers between devices with their start and end apart: 2, of which 1 were waited for; matrix products, arithmetic and copies ran while one was open for 0% of the time, Pallas kernels for 16%

profile of v1, /device:TPU:0, one launch (start us, length us, event | category | flops | bytes accessed | tf_op | source)
XLA Modules:
  0.0 92.3 jit_solution(14208655102552693137)
XLA Ops:
  0.6 0.0 copy-start.1
  0.6 0.9 copy-done.1
  1.5 0.0 copy-start.3
  1.5 0.9 copy-done.3
  2.4 0.7 copy-done.5
  3.1 0.6 pack.1
  3.7 19.2 %all_to_all.20.held_ref = bf16[32,40,128]{2,1,0:T(8,128)(2,1)S(1)} all-to-all(bf16[32,40,128]{2,1,0:T(8,128)(2,1)S(1)} %pack.1), channel_id=1, replica_groups=mesh['cp'=32] {'cp'}, dimensions={0} | all-to-all | bytes 655360 | tf_op jit(solution)/shard_map/all_to_all | solution.py:237
  22.9 1.9 %gather.1 = (bf16[32,2,32,128]{3,2,1,0:T(8,128)(2,1)}, s32[32,128]{1,0:T(8,128)S(1)}) custom-call(bf16[32,40,128]{2,1,0:T(8,128)(2,1)S(1)} %all_to_all.20.held_ref), custom_call_target="tpu_custom_call" | custom-call | flops 1000000 | bytes 1024 | tf_op jit(solution)/shard_map/gather/pallas_call | solution.py:268
  24.7 0.0 copy-start.2
  24.7 0.0 copy-start.4
  24.7 0.0 copy-start.6
  24.7 2.8 %all-to-all-start.1 = ((bf16[32,2,32,128]{3,2,1,0:T(8,128)(2,1)}), bf16[32,2,32,128]{3,2,1,0:T(8,128)(2,1)S(1)}, u32[]{:S(2)}, u32[]{:S(2)}) async-start(bf16[32,2,32,128]{3,2,1,0:T(8,128)(2,1)} %get-tuple-element.20), calls=%async_computation.1 | async-start | bytes 1048576 | tf_op jit(solution)/shard_map/all_to_all | solution.py:237
  27.5 0.0 copy-done.7
  27.5 0.0 copy-done.2
  27.5 0.0 copy-done.4
  27.5 0.0 copy-done.6
  27.6 1.5 %pre.1 = (bf16[4,128,512]{2,1,0:T(8,128)(2,1)S(1)}, bf16[4,128,512]{2,1,0:T(8,128)(2,1)S(1)}, f32[4,8,512]{2,1,0:T(8,128)S(1)}) custom-call(bf16[512,512]{1,0:T(8,128)(2,1)S(1)} %copy-done.6, bf16[512,512]{1,0:T(8,128)(2,1)S(1)} %copy-done.7, bf16[512,128]{1,0:T(8,128)(2,1)S(1)} %copy-done.2, bf16[512,128]{1,0:T(8,128)(2,1)S(1)} %copy-done.4), custom_call_target="tpu_custom_call" | custom-call | flops 536870912 | bytes 1024 | tf_op jit(solution)/shard_map/pre/pallas_call | solution.py:259
  29.0 0.0 copy-start.8
  29.1 0.8 copy-done.8
  29.8 0.8 copy-done.9
  30.6 0.6 copy-done.10
  31.3 11.9 %all-to-all-done.1.fetched_ref = bf16[32,2,32,128]{3,2,1,0:T(8,128)(2,1)S(1)} async-done(((bf16[32,2,32,128]{3,2,1,0:T(8,128)(2,1)}), bf16[32,2,32,128]{3,2,1,0:T(8,128)(2,1)S(1)}, u32[]{:S(2)}, u32[]{:S(2)}) %all-to-all-start.1) | async-done | bytes 524320 | tf_op jit(solution)/shard_map/all_to_all | solution.py:237
  43.1 0.8 copy-done.11
  43.9 10.1 %main.1 = (bf16[32,2,32,128]{3,2,1,0:T(8,128)(2,1)}, f32[4,8,512]{2,1,0:T(8,128)}) custom-call(s32[1,2]{1,0:T(1,128)} %sel_ref.5, bf16[32,2,32,128]{3,2,1,0:T(8,128)(2,1)} %copy-done.11, bf16[4,128,512]{2,1,0:T(8,128)(2,1)} %copy-done.8, bf16[4,128,512]{2,1,0:T(8,128)(2,1)} %copy-done.9, bf16[512,512]{1,0:T(8,128)(2,1)} %queries_ref.5, ...), custom_call_target="tpu_custom_call" | custom-call | flops 2147483648 | bytes 1024 | tf_op jit(solution)/shard_map/main/pallas_call | solution.py:279
  54.0 18.5 %all_to_all.21.received_ref = bf16[32,2,32,128]{3,2,1,0:T(8,128)(2,1)S(1)} all-to-all(bf16[32,2,32,128]{3,2,1,0:T(8,128)(2,1)} %get-tuple-element.28), channel_id=1, replica_groups=mesh['cp'=32] {'cp'}, dimensions={0} | all-to-all | bytes 1048576 | tf_op jit(solution)/shard_map/all_to_all | solution.py:237
  72.5 1.9 %sum.1 = bf16[32,32,128]{2,1,0:T(8,128)(2,1)} custom-call(s32[32,128]{1,0:T(8,128)S(1)} %get-tuple-element.27.ids_ref, bf16[32,2,32,128]{3,2,1,0:T(8,128)(2,1)S(1)} %all_to_all.21.received_ref), custom_call_target="tpu_custom_call" | custom-call | flops 1000000 | bytes 1024 | tf_op jit(solution)/shard_map/sum/pallas_call | solution.py:299
  74.4 3.2 %all-to-all-start.3 = ((bf16[32,32,128]{2,1,0:T(8,128)(2,1)}), bf16[32,32,128]{2,1,0:T(8,128)(2,1)S(1)}, u32[]{:S(2)}, u32[]{:S(2)}) async-start(bf16[32,32,128]{2,1,0:T(8,128)(2,1)} %sum.1), calls=%async_computation.3 | async-start | bytes 524288 | tf_op jit(solution)/shard_map/all_to_all | solution.py:237
  77.5 6.7 %selected.1 = (f32[4,128,512]{2,1,0:T(8,128)}, f32[4,128,512]{2,1,0:T(8,128)}) custom-call(s32[1,2]{1,0:T(1,128)} %sel_ref.5, bf16[32,2,32,128]{3,2,1,0:T(8,128)(2,1)} %copy-done.11, bf16[4,128,512]{2,1,0:T(8,128)(2,1)} %copy-done.8, bf16[4,128,512]{2,1,0:T(8,128)(2,1)} %copy-done.9, f32[4,8,512]{2,1,0:T(8,128)} %get-tuple-element.22.stats_ref), custom_call_target="tpu_custom_call" | custom-call | flops 2147483648 | bytes 1024 | tf_op jit(solution)/shard_map/selected/pallas_call | solution.py:290
  84.2 6.3 %own.1 = (bf16[512,512]{1,0:T(8,128)(2,1)}, bf16[512,512]{1,0:T(8,128)(2,1)}, f32[1024,128]{1,0:T(8,128)}) custom-call(bf16[512,128]{1,0:T(8,128)(2,1)} %keys_ref.5, bf16[512,128]{1,0:T(8,128)(2,1)} %values_ref.5, bf16[4,128,512]{2,1,0:T(8,128)(2,1)} %copy-done.8, bf16[4,128,512]{2,1,0:T(8,128)(2,1)} %copy-done.9, bf16[512,512]{1,0:T(8,128)(2,1)} %queries_ref.5, ...), custom_call_target="tpu_custom_call" | custom-call | flops 1610612736 | bytes 1024 | tf_op jit(solution)/shard_map/own/pallas_call | solution.py:310
  90.6 0.0 all-to-all-done.3.returned_ref
  90.6 1.0 %copy-done = f32[1024,128]{1,0:T(8,128)S(1)} copy-done((f32[1024,128]{1,0:T(8,128)S(1)}, f32[1024,128]{1,0:T(8,128)}, u32[]{:S(2)}) %copy-start) | copy-done | bytes 524312
  91.6 0.7 final.1
  (6 shorter events, 0.0 us)
Async XLA Ops:
  0.6 0.9 copy-start.1
  1.5 0.9 copy-start.3
  2.4 0.7 copy-start.5
  22.8 4.7 %copy-start.7 = (bf16[512,512]{1,0:T(8,128)(2,1)S(1)}, bf16[512,512]{1,0:T(8,128)(2,1)}, u32[]{:S(2)}) copy-start(bf16[512,512]{1,0:T(8,128)(2,1)} %grad_ref.5) | copy-start | bytes 1572868
  24.7 2.8 %copy-start.2 = (bf16[512,128]{1,0:T(8,128)(2,1)S(1)}, bf16[512,128]{1,0:T(8,128)(2,1)}, u32[]{:S(2)}) copy-start(bf16[512,128]{1,0:T(8,128)(2,1)} %keys_ref.5) | copy-start | bytes 393220
  24.7 2.8 %copy-start.4 = (bf16[512,128]{1,0:T(8,128)(2,1)S(1)}, bf16[512,128]{1,0:T(8,128)(2,1)}, u32[]{:S(2)}) copy-start(bf16[512,128]{1,0:T(8,128)(2,1)} %values_ref.5) | copy-start | bytes 393220
  24.7 2.8 %copy-start.6 = (bf16[512,512]{1,0:T(8,128)(2,1)S(1)}, bf16[512,512]{1,0:T(8,128)(2,1)}, u32[]{:S(2)}) copy-start(bf16[512,512]{1,0:T(8,128)(2,1)} %queries_ref.5) | copy-start | bytes 1572868
  24.7 18.4 %all-to-all-start.1 = ((bf16[32,2,32,128]{3,2,1,0:T(8,128)(2,1)}), bf16[32,2,32,128]{3,2,1,0:T(8,128)(2,1)S(1)}, u32[]{:S(2)}, u32[]{:S(2)}) async-start(bf16[32,2,32,128]{3,2,1,0:T(8,128)(2,1)} %get-tuple-element.20), calls=%async_computation.1 | async-start | bytes 1048576 | tf_op jit(solution)/shard_map/all_to_all | solution.py:237
  29.0 0.8 copy-start.8
  29.8 0.8 copy-start.9
  30.6 0.6 copy-start.10
  43.1 0.8 copy-start.11
  74.4 16.2 %all-to-all-start.3 = ((bf16[32,32,128]{2,1,0:T(8,128)(2,1)}), bf16[32,32,128]{2,1,0:T(8,128)(2,1)S(1)}, u32[]{:S(2)}, u32[]{:S(2)}) async-start(bf16[32,32,128]{2,1,0:T(8,128)(2,1)} %sum.1), calls=%async_computation.3 | async-start | bytes 524288 | tf_op jit(solution)/shard_map/all_to_all | solution.py:237
  90.6 1.0 %copy-start = (f32[1024,128]{1,0:T(8,128)S(1)}, f32[1024,128]{1,0:T(8,128)}, u32[]{:S(2)}) copy-start(f32[1024,128]{1,0:T(8,128)} %get-tuple-element.29.own_ref) | copy-start | bytes 1572868

commit v2 on v1

--- a/solution.py
+++ b/solution.py
@@ -1,11 +1,10 @@
-import functools
-
 import jax
 import jax.numpy as jnp
 from jax import lax
 from jax.experimental import pallas as pl
 from jax.experimental.pallas import tpu as pltpu
 from jax.sharding import PartitionSpec as P
+
 
 HEADS = 4
 HEAD_DIM = 128
@@ -16,6 +15,8 @@
 LOG2_SCALE = SCALE * 1.4426950408889634
 MASKED = -1e30
 
+WHOLE_VMEM = 67_000_000
+
 f32 = jnp.float32
 bf16 = jnp.bfloat16
 
@@ -32,7 +33,11 @@
     return pl.BlockSpec(memory_space=pltpu.SMEM)
 
 
-def params(mib=40):
+def hbm():
+    return pl.BlockSpec(memory_space=pltpu.HBM)
+
+
+def params(mib=16):
     return pltpu.CompilerParams(vmem_limit_bytes=mib * 1024 * 1024)
 
 
@@ -40,20 +45,29 @@
     return pl.CostEstimate(flops=flops, transcendentals=trans, bytes_accessed=nbytes)
 
 
-def pack_kernel(sel_ref, keys_ref, values_ref, out_ref):
+def pack_kernel(sel_ref, keys_ref, values_ref, out_ref, sel_smem, sems):
     parts, rows, width = out_ref.shape
     rows = rows - SUB
     half = parts // 2
-    out_ref[:half, :rows, :] = keys_ref[...].reshape(half, rows, width)
-    out_ref[half:, :rows, :] = values_ref[...].reshape(half, rows, width)
+    copies = [
+        pltpu.make_async_copy(keys_ref, out_ref.at[:half, :rows, :], sems.at[0]),
+        pltpu.make_async_copy(values_ref, out_ref.at[half:, :rows, :], sems.at[1]),
+    ]
+    chosen = pltpu.make_async_copy(sel_ref, sel_smem, sems.at[2])
+    chosen.start()
+    for copy in copies:
+        copy.start()
+    chosen.wait()
     lane = lax.broadcasted_iota(jnp.int32, (SUB, width), 1)
     ids = jnp.zeros((SUB, width), jnp.int32)
     for slot in range(2):
-        number = sel_ref[0, slot] + 1
+        number = sel_smem[0, slot] + 1
         ids = jnp.where(lane == 2 * slot, lax.shift_right_logical(number, 7), ids)
         ids = jnp.where(lane == 2 * slot + 1, number & (DIGIT - 1), ids)
     tail = ids.astype(f32).astype(bf16)
     out_ref[:, rows:, :] = jnp.broadcast_to(tail[None], (parts, SUB, width))
+    for copy in copies:
+        copy.wait()
 
 
 def request_of(ids_ref, reader, slot):
@@ -61,7 +75,7 @@
 
 
 def gather_kernel(held_ref, out_ref, ids_ref, ids_smem, sem):
-    readers, _, rows, width = out_ref.shape
+    readers, _, rows, _ = out_ref.shape
     tail = held_ref[:, rows:, :].astype(f32)
     ids_ref[...] = jnp.max(tail, axis=1).astype(jnp.int32)
     copy = pltpu.make_async_copy(ids_ref, ids_smem, sem)
@@ -77,7 +91,7 @@
     lax.fori_loop(0, readers, one, 0, unroll=8)
 
 
-def pre_kernel(queries_ref, grad_ref, keys_ref, values_ref, qt_ref, gt_ref, stats_ref):
+def pre_kernel(sel_ref, queries_ref, grad_ref, keys_ref, values_ref, qt_ref, gt_ref, stats_ref):
     keys = keys_ref[...]
     values = values_ref[...]
     key_at = lax.broadcasted_iota(jnp.int32, (BLK, BLK), 0)
@@ -95,69 +109,91 @@
         stats_ref[h, 0:1, :] = top
         stats_ref[h, 1:2, :] = jnp.sum(weight, axis=0, keepdims=True)
         stats_ref[h, 2:3, :] = jnp.sum(weight * dot(values, gt), axis=0, keepdims=True)
-
-
-def slot_terms(sel_ref, slot):
-    ok = sel_ref[0, slot] >= 0
-    return jnp.where(ok, 1.0, 0.0), jnp.where(ok, 0.0, 1e30), jnp.where(ok, 0.0, MASKED)
-
-
-def main_kernel(sel_ref, fetched_ref, qt_ref, gt_ref, queries_ref, grad_ref, own_ref, out_ref, stats_ref):
+        for slot in range(2):
+            keep = jnp.where(sel_ref[0, slot] >= 0, 1.0, 0.0)
+            stats_ref[h, 3 + slot : 4 + slot, :] = jnp.full((1, BLK), keep, f32)
+
+
+def slot_terms(stats_ref, slot):
+    keep = stats_ref[0, 3 + slot : 4 + slot, :]
+    return keep, (1.0 - keep) * 1e30
+
+
+def main_kernel(
+    fetched_ref, qt_ref, gt_ref, queries_ref, grad_ref, own_ref, out_ref, stats_ref, score_ref, gp_ref, low_ref, ds_ref
+):
     parts, _, rows, width = fetched_ref.shape
     half = parts // 2
+    step = 128
+    count = 2 * BLK // step
     keys = [fetched_ref[:half, s].reshape(BLK, width) for s in range(2)]
     values = [fetched_ref[half:, s].reshape(BLK, width) for s in range(2)]
-    terms = [slot_terms(sel_ref, s) for s in range(2)]
-    grad_k = [None, None]
-    grad_v = [None, None]
+    terms = [slot_terms(own_ref, s) for s in range(2)]
+
+    def at(c):
+        return slice(c * step, (c + 1) * step)
+
+    def piece(blocks, c):
+        s, first = divmod(c * step, BLK)
+        return blocks[s][first : first + step, :]
+
+    def fold(x, reduce):
+        return reduce(x.reshape(step // SUB, SUB, BLK), axis=0)
+
     for h in range(HEADS):
-        cols = slice(h * HEAD_DIM, (h + 1) * HEAD_DIM)
+        wide = slice(h * BLK, (h + 1) * BLK)
+        buf = h % 2
         qt = qt_ref[h]
         gt = gt_ref[h]
-        q_h = queries_ref[:, cols]
-        g_h = grad_ref[:, cols]
+        tops = [None, None]
+        for c in range(count):
+            s = c * step // BLK
+            x = dot(piece(keys, c), qt)
+            score_ref[buf, at(c), :] = x
+            m = fold(x, jnp.max)
+            tops[s] = m if tops[s] is None else jnp.maximum(tops[s], m)
+        for c in range(count):
+            gp_ref[buf, at(c), :] = dot(piece(values, c), gt)
         top0 = own_ref[h, 0:1, :]
-        scores = [dot(keys[s], qt) for s in range(2)]
         top = top0
         for s in range(2):
-            _, _, low = terms[s]
-            keep, _, _ = terms[s]
-            top = jnp.maximum(top, jnp.max(scores[s], axis=0, keepdims=True) * keep + low)
+            keep, far = terms[s]
+            top = jnp.maximum(top, jnp.max(tops[s], axis=0, keepdims=True) * keep - far)
         base = top * LOG2_SCALE
         alpha = jnp.exp2(top0 * LOG2_SCALE - base)
-        total = own_ref[h, 1:2, :] * alpha
-        inner = own_ref[h, 2:3, :] * alpha
-        weight = []
-        for s in range(2):
-            keep, high, _ = terms[s]
-            w = jnp.exp2(scores[s] * (keep * LOG2_SCALE) - (base * keep + high))
-            weight.append(w)
-            total = total + jnp.sum(w, axis=0, keepdims=True)
+        total8 = None
+        inner8 = None
+        for c in range(count):
+            keep, far = terms[c * step // BLK]
+            w = jnp.exp2(score_ref[buf, at(c), :] * (keep * LOG2_SCALE) - (base * keep + far))
+            score_ref[buf, at(c), :] = w
+            t = fold(w, jnp.sum)
+            i = fold(w * gp_ref[buf, at(c), :], jnp.sum)
+            total8 = t if total8 is None else total8 + t
+            inner8 = i if inner8 is None else inner8 + i
+        total = own_ref[h, 1:2, :] * alpha + jnp.sum(total8, axis=0, keepdims=True)
         inverse = 1.0 / total
-        inner = inner * inverse
-        grads = []
-        for s in range(2):
-            weight[s] = weight[s] * inverse
-            grads.append(dot(values[s], gt))
-            inner = inner + jnp.sum(weight[s] * grads[s], axis=0, keepdims=True)
-        for s in range(2):
-            dv = dot(weight[s].astype(bf16), g_h)
-            grad_v[s] = dv if grad_v[s] is None else grad_v[s] + dv
-            ds = (weight[s] * (grads[s] - inner)).astype(bf16)
-            dk = dot(ds, q_h)
-            grad_k[s] = dk if grad_k[s] is None else grad_k[s] + dk
+        inner = (own_ref[h, 2:3, :] * alpha + jnp.sum(inner8, axis=0, keepdims=True)) * inverse
+        for c in range(count):
+            w = score_ref[buf, at(c), :] * inverse
+            low_ref[at(c), wide] = w.astype(bf16)
+            ds_ref[at(c), wide] = (w * (gp_ref[buf, at(c), :] - inner)).astype(bf16)
         stats_ref[h, 0:1, :] = base
         stats_ref[h, 1:2, :] = inverse
         stats_ref[h, 2:3, :] = inner
+        stats_ref[h, 3:5, :] = own_ref[h, 3:5, :]
+    q_tall = jnp.concatenate([queries_ref[:, h * HEAD_DIM : (h + 1) * HEAD_DIM] for h in range(HEADS)], axis=0)
+    g_tall = jnp.concatenate([grad_ref[:, h * HEAD_DIM : (h + 1) * HEAD_DIM] for h in range(HEADS)], axis=0)
     for s in range(2):
-        out_ref[:half, s] = (grad_k[s] * SCALE).astype(bf16).reshape(half, rows, width)
-        out_ref[half:, s] = grad_v[s].astype(bf16).reshape(half, rows, width)
-
-
-def selected_kernel(sel_ref, fetched_ref, qt_ref, gt_ref, stats_ref, att_ref, dq_ref):
-    parts, _, rows, width = fetched_ref.shape
+        block = slice(s * BLK, (s + 1) * BLK)
+        out_ref[half:, s] = dot(low_ref[block, :], g_tall).astype(bf16).reshape(half, rows, width)
+        out_ref[:half, s] = (dot(ds_ref[block, :], q_tall) * SCALE).astype(bf16).reshape(half, rows, width)
+
+
+def selected_kernel(fetched_ref, qt_ref, gt_ref, stats_ref, att_ref, dq_ref):
+    parts, _, _, width = fetched_ref.shape
     half = parts // 2
-    terms = [slot_terms(sel_ref, s) for s in range(2)]
+    terms = [slot_terms(stats_ref, s) for s in range(2)]
     keys = [fetched_ref[:half, s].reshape(BLK, width) for s in range(2)]
     values = [fetched_ref[half:, s].reshape(BLK, width) for s in range(2)]
     keys_t = [k.T for k in keys]
@@ -169,9 +205,9 @@
         att = None
         dq = None
         for s in range(2):
-            keep, high, _ = terms[s]
+            keep, far = terms[s]
             scores = dot(keys[s], qt_ref[h])
-            w = jnp.exp2(scores * (keep * LOG2_SCALE) - (base * keep + high)) * inverse
+            w = jnp.exp2(scores * (keep * LOG2_SCALE) - (base * keep + far)) * inverse
             ds = (w * (dot(values[s], gt_ref[h]) - inner)).astype(bf16)
             att_s = dot(values_t[s], w.astype(bf16))
             dq_s = dot(keys_t[s], ds)
@@ -212,13 +248,16 @@
     own_out[BLK:, :] = grad_v
 
 
-def sum_kernel(ids_ref, received_ref, out_ref, acc_ref):
+def sum_kernel(ids_ref, received_ref, out_ref, acc_ref, ids_smem, sem):
     readers = received_ref.shape[0]
+    copy = pltpu.make_async_copy(ids_ref, ids_smem, sem)
+    copy.start()
     acc_ref[...] = jnp.zeros(acc_ref.shape, f32)
+    copy.wait()
 
     def one(reader, carry):
         for slot in range(2):
-            block = jnp.maximum(request_of(ids_ref, reader, slot), 0)
+            block = jnp.maximum(request_of(ids_smem, reader, slot), 0)
             acc_ref[block] = acc_ref[block] + received_ref[reader, slot].astype(f32)
         return carry
 
@@ -227,7 +266,7 @@
 
 
 def final_kernel(returned_ref, own_ref, dk_ref, dv_ref):
-    parts, rows, width = returned_ref.shape
+    parts, _, width = returned_ref.shape
     half = parts // 2
     dk_ref[...] = (returned_ref[:half].reshape(BLK, width).astype(f32) + own_ref[:BLK, :]).astype(bf16)
     dv_ref[...] = (returned_ref[half:].reshape(BLK, width).astype(f32) + own_ref[BLK:, :]).astype(bf16)
@@ -247,24 +286,25 @@
     packed = pl.pallas_call(
         pack_kernel,
         out_shape=shape((parts, rows + SUB, width), bf16),
-        in_specs=[smem(), vmem(), vmem()],
+        in_specs=[hbm(), hbm(), hbm()],
         out_specs=vmem(),
-        compiler_params=params(),
+        scratch_shapes=[pltpu.SMEM((1, 2), jnp.int32), pltpu.SemaphoreType.DMA((3,))],
+        compiler_params=pltpu.CompilerParams(vmem_limit_bytes=WHOLE_VMEM),
         cost_estimate=cost(1000000),
         name="pack",
-    )(selections, keys, values)
+    )(selections, keys.reshape(parts // 2, rows, width), values.reshape(parts // 2, rows, width))
     held = exchange(packed)
     heads_t = shape((HEADS, HEAD_DIM, BLK), bf16)
     stats = shape((HEADS, SUB, BLK), f32)
     q_t, g_t, own_stats = pl.pallas_call(
         pre_kernel,
         out_shape=(heads_t, heads_t, stats),
-        in_specs=[vmem()] * 4,
+        in_specs=[smem()] + [vmem()] * 4,
         out_specs=(vmem(),) * 3,
         compiler_params=params(),
         cost_estimate=cost(2 * unit, HEADS * BLK * BLK),
         name="pre",
-    )(queries, grad_out, keys, values)
+    )(selections, queries, grad_out, keys, values)
     outgoing, ids = pl.pallas_call(
         gather_kernel,
         out_shape=(shape((parts, 2, rows, width), bf16), shape((parts, width), jnp.int32)),
@@ -279,29 +319,39 @@
     partial, full_stats = pl.pallas_call(
         main_kernel,
         out_shape=(shape((parts, 2, rows, width), bf16), stats),
-        in_specs=[smem()] + [vmem()] * 6,
+        in_specs=[vmem()] * 6,
         out_specs=(vmem(), vmem()),
-        compiler_params=params(56),
+        scratch_shapes=[
+            pltpu.VMEM((2, 2 * BLK, BLK), f32),
+            pltpu.VMEM((2, 2 * BLK, BLK), f32),
+            pltpu.VMEM((2 * BLK, HEADS * BLK), bf16),
+            pltpu.VMEM((2 * BLK, HEADS * BLK), bf16),
+        ],
+        compiler_params=params(28),
         cost_estimate=cost(8 * unit, 2 * HEADS * BLK * BLK),
         name="main",
-    )(selections, fetched, q_t, g_t, queries, grad_out, own_stats)
+    )(fetched, q_t, g_t, queries, grad_out, own_stats)
     received = exchange(partial)
     acc_t = shape((HEADS, HEAD_DIM, BLK), f32)
     att_t, dq_t = pl.pallas_call(
         selected_kernel,
         out_shape=(acc_t, acc_t),
-        in_specs=[smem()] + [vmem()] * 4,
+        in_specs=[vmem()] * 4,
         out_specs=(vmem(), vmem()),
-        compiler_params=params(56),
+        compiler_params=params(28),
         cost_estimate=cost(8 * unit, 2 * HEADS * BLK * BLK),
         name="selected",
-    )(selections, fetched, q_t, g_t, full_stats)
+    )(fetched, q_t, g_t, full_stats)
     summed = pl.pallas_call(
         sum_kernel,
         out_shape=shape((parts, rows, width), bf16),
-        in_specs=[smem(), vmem()],
+        in_specs=[vmem(), vmem()],
         out_specs=vmem(),
-        scratch_shapes=[pltpu.VMEM((parts, rows, width), f32)],
+        scratch_shapes=[
+            pltpu.VMEM((parts, rows, width), f32),
+            pltpu.SMEM((parts, width), jnp.int32),
+            pltpu.SemaphoreType.DMA,
+        ],
         compiler_params=params(),
         cost_estimate=cost(1000000),
         name="sum",
@@ -312,7 +362,7 @@
         out_shape=(shape((BLK, HEADS * HEAD_DIM), bf16), shape((BLK, HEADS * HEAD_DIM), bf16), shape((2 * BLK, width), f32)),
         in_specs=[vmem()] * 9,
         out_specs=(vmem(),) * 3,
-        compiler_params=params(56),
+        compiler_params=params(28),
         cost_estimate=cost(6 * unit, HEADS * BLK * BLK),
         name="own",
     )(keys, values, q_t, g_t, queries, grad_out, full_stats, att_t, dq_t)

time: 92.8 us -> 84 us (0.905)
  local copies, waits for them, and re-layouts: 6.52 us -> 0.03 us
  Pallas kernels: 29.6 us -> 23.2 us
  waiting for transfers between devices: 11.9 us -> 16 us
    unnamed x24 -> x10, local copies, waits for them, and re-layouts: 6.52 us -> 0.03 us
    all_to_all x2, waiting for transfers between devices: 11.9 us -> 16 us  [exchange(): return lax.all_to_all(array, 'cp', split_axis=0, concat_axis=0, tiled=True)]
    pallas_call x1, Pallas kernels: 10.1 us -> 7.11 us  [body(): pl.pallas_call(main_kernel, out_shape=(shape((parts, 2, rows, width), bf1...]
    pallas_call x1, Pallas kernels: 6.68 us -> 4.06 us  [body(): pl.pallas_call(selected_kernel, out_shape=(acc_t, acc_t), in_specs=[vmem(...]
    pallas_call x1, Pallas kernels: 6.35 us -> 3.87 us  [body(): pl.pallas_call(own_kernel, out_shape=(shape((BLK, HEADS * HEAD_DIM), bf16...]
    pallas_call x1, Pallas kernels: 0.57 us -> 1.72 us  [body(): pl.pallas_call(pack_kernel, out_shape=shape((parts, rows + SUB, width), b...]
  transfers between devices with their start and end apart: 2 -> 2, of which waited for: 1 -> 2; matrix products, arithmetic and copies ran while one was open for 0% -> 0% of each run, Pallas kernels for 16% -> 12%
where the time goes in v2:
time: 84 us; the launch traced here: 83.6 us
  blocking collectives  37.7 us (45%)
  Pallas kernels  23.2 us (28%)
  waiting for transfers between devices  16 us (19%)
  starting transfers between devices  5.92 us (7%)
    all_to_all x2, blocking collectives, exchange(): return lax.all_to_all(array, 'cp', split_axis=0, concat_axis=0, tiled=True)  37.7 us
    all_to_all x2, waiting for transfers between devices, exchange(): return lax.all_to_all(array, 'cp', split_axis=0, concat_axis=0, tiled=True)  16 us
    pallas_call x1, Pallas kernels, body(): pl.pallas_call(main_kernel, out_shape=(shape((parts, 2, rows, width), bf1...  7.11 us
    all_to_all x2, starting transfers between devices, exchange(): return lax.all_to_all(array, 'cp', split_axis=0, concat_axis=0, tiled=True)  5.92 us
    pallas_call x1, Pallas kernels, body(): pl.pallas_call(selected_kernel, out_shape=(acc_t, acc_t), in_specs=[vmem(...  4.06 us
    pallas_call x1, Pallas kernels, body(): pl.pallas_call(own_kernel, out_shape=(shape((BLK, HEADS * HEAD_DIM), bf16...  3.87 us
    pallas_call x1, Pallas kernels, body(): pl.pallas_call(pre_kernel, out_shape=(heads_t, heads_t, stats), in_specs=...  2.03 us
    pallas_call x1, Pallas kernels, body(): pl.pallas_call(sum_kernel, out_shape=shape((parts, rows, width), bf16), i...  1.87 us
  transfers between devices with their start and end apart: 2, of which 2 were waited for; matrix products, arithmetic and copies ran while one was open for 0% of the time, Pallas kernels for 12%

profile of v2, /device:TPU:0, one launch (start us, length us, event | category | flops | bytes accessed | tf_op | source)
XLA Modules:
  0.0 83.6 jit_solution(9021448054992359294)
XLA Ops:
  0.6 1.7 %pack.1 = bf16[32,40,128]{2,1,0:T(8,128)(2,1)} custom-call(s32[1,2]{1,0:T(1,128)} %sel_ref.3, bf16[16,32,128]{2,1,0:T(8,128)(2,1)} %bitcast.2, bf16[16,32,128]{2,1,0:T(8,128)(2,1)} %bitcast.3), custom_call_target="tpu_custom_call" | custom-call | flops 1000000 | bytes 1024 | tf_op jit(solution)/shard_map/pack/pallas_call | solution.py:286
  2.4 19.4 %all_to_all.20.held_ref = bf16[32,40,128]{2,1,0:T(8,128)(2,1)S(1)} all-to-all(bf16[32,40,128]{2,1,0:T(8,128)(2,1)} %pack.1), channel_id=1, replica_groups=mesh['cp'=32] {'cp'}, dimensions={0} | all-to-all | bytes 655360 | tf_op jit(solution)/shard_map/all_to_all | solution.py:276
  21.7 0.0 copy-start.4
  21.7 1.9 %gather.1 = (bf16[32,2,32,128]{3,2,1,0:T(8,128)(2,1)}, s32[32,128]{1,0:T(8,128)S(1)}) custom-call(bf16[32,40,128]{2,1,0:T(8,128)(2,1)S(1)} %all_to_all.20.held_ref), custom_call_target="tpu_custom_call" | custom-call | flops 1000000 | bytes 1024 | tf_op jit(solution)/shard_map/gather/pallas_call | solution.py:308
  23.6 0.0 copy-start
  23.6 0.0 copy-start.1
  23.6 0.0 copy-start.2
  23.6 0.0 copy-start.3
  23.7 2.8 %all-to-all-start.1 = ((bf16[32,2,32,128]{3,2,1,0:T(8,128)(2,1)}), bf16[32,2,32,128]{3,2,1,0:T(8,128)(2,1)S(1)}, u32[]{:S(2)}, u32[]{:S(2)}) async-start(bf16[32,2,32,128]{3,2,1,0:T(8,128)(2,1)} %get-tuple-element.20), calls=%async_computation.1 | async-start | bytes 1048576 | tf_op jit(solution)/shard_map/all_to_all | solution.py:276
  26.4 0.0 copy-done.4
  26.4 0.0 copy-done
  26.4 0.0 copy-done.1
  26.5 0.0 copy-done.2
  26.5 0.0 copy-done.3
  26.5 2.0 %pre.1 = (bf16[4,128,512]{2,1,0:T(8,128)(2,1)S(1)}, bf16[4,128,512]{2,1,0:T(8,128)(2,1)S(1)}, f32[4,8,512]{2,1,0:T(8,128)S(1)}) custom-call(s32[1,2]{1,0:T(1,128)S(1)} %copy-done.2, bf16[512,512]{1,0:T(8,128)(2,1)S(1)} %copy-done.3, bf16[512,512]{1,0:T(8,128)(2,1)S(1)} %copy-done.4, bf16[512,128]{1,0:T(8,128)(2,1)S(1)} %copy-done, bf16[512,128]{1,0:T(8,128)(2,1)S(1)} %copy-done.1), custom_call_target="tpu_custom_call" | custom-call | flops 536870912 | bytes 1024 | tf_op jit(solution)/shard_map/pre/pallas_call | solution.py:299
  28.5 13.5 %all-to-all-done.1.fetched_ref = bf16[32,2,32,128]{3,2,1,0:T(8,128)(2,1)S(1)} async-done(((bf16[32,2,32,128]{3,2,1,0:T(8,128)(2,1)}), bf16[32,2,32,128]{3,2,1,0:T(8,128)(2,1)S(1)}, u32[]{:S(2)}, u32[]{:S(2)}) %all-to-all-start.1) | async-done | bytes 524320 | tf_op jit(solution)/shard_map/all_to_all | solution.py:276
  42.0 7.1 %main.1 = (bf16[32,2,32,128]{3,2,1,0:T(8,128)(2,1)S(1)}, f32[4,8,512]{2,1,0:T(8,128)S(1)}) custom-call(bf16[32,2,32,128]{3,2,1,0:T(8,128)(2,1)S(1)} %all-to-all-done.1.fetched_ref, bf16[4,128,512]{2,1,0:T(8,128)(2,1)S(1)} %get-tuple-element.18.qt_ref, bf16[4,128,512]{2,1,0:T(8,128)(2,1)S(1)} %get-tuple-element.19.gt_ref, bf16[512,512]{1,0:T(8,128)(2,1)S(1)} %copy-done.3, ...), custom_call_target="tpu_custom_call" | custom-call | flops 2147483648 | bytes 1024 | tf_op jit(solution)/shard_map/main/pallas_call | solution.py:319
  49.2 18.3 %all_to_all.21.received_ref = bf16[32,2,32,128]{3,2,1,0:T(8,128)(2,1)S(1)} all-to-all(bf16[32,2,32,128]{3,2,1,0:T(8,128)(2,1)S(1)} %get-tuple-element.28), channel_id=1, replica_groups=mesh['cp'=32] {'cp'}, dimensions={0} | all-to-all | bytes 1048576 | tf_op jit(solution)/shard_map/all_to_all | solution.py:276
  67.5 1.9 %sum.1 = bf16[32,32,128]{2,1,0:T(8,128)(2,1)} custom-call(s32[32,128]{1,0:T(8,128)S(1)} %get-tuple-element.27.ids_ref, bf16[32,2,32,128]{3,2,1,0:T(8,128)(2,1)S(1)} %all_to_all.21.received_ref), custom_call_target="tpu_custom_call" | custom-call | flops 1000000 | bytes 1024 | tf_op jit(solution)/shard_map/sum/pallas_call | solution.py:345
  69.3 3.2 %all-to-all-start.3 = ((bf16[32,32,128]{2,1,0:T(8,128)(2,1)}), bf16[32,32,128]{2,1,0:T(8,128)(2,1)S(1)}, u32[]{:S(2)}, u32[]{:S(2)}) async-start(bf16[32,32,128]{2,1,0:T(8,128)(2,1)} %sum.1), calls=%async_computation.3 | async-start | bytes 524288 | tf_op jit(solution)/shard_map/all_to_all | solution.py:276
  72.5 4.1 %selected.1 = (f32[4,128,512]{2,1,0:T(8,128)S(1)}, f32[4,128,512]{2,1,0:T(8,128)S(1)}) custom-call(bf16[32,2,32,128]{3,2,1,0:T(8,128)(2,1)S(1)} %all-to-all-done.1.fetched_ref, bf16[4,128,512]{2,1,0:T(8,128)(2,1)S(1)} %get-tuple-element.18.qt_ref, bf16[4,128,512]{2,1,0:T(8,128)(2,1)S(1)} %get-tuple-element.19.gt_ref, ...), custom_call_target="tpu_custom_call" | custom-call | flops 2147483648 | bytes 1024 | tf_op jit(solution)/shard_map/selected/pallas_call | solution.py:336
  76.6 3.9 %own.1 = (bf16[512,512]{1,0:T(8,128)(2,1)}, bf16[512,512]{1,0:T(8,128)(2,1)}, f32[1024,128]{1,0:T(8,128)S(1)}) custom-call(bf16[512,128]{1,0:T(8,128)(2,1)S(1)} %copy-done, bf16[512,128]{1,0:T(8,128)(2,1)S(1)} %copy-done.1, bf16[4,128,512]{2,1,0:T(8,128)(2,1)S(1)} %get-tuple-element.18.qt_ref, bf16[4,128,512]{2,1,0:T(8,128)(2,1)S(1)} %get-tuple-element.19.gt_ref, ...), custom_call_target="tpu_custom_call" | custom-call | flops 1610612736 | bytes 1024 | tf_op jit(solution)/shard_map/own/pallas_call | solution.py:360
  80.4 2.5 %all-to-all-done.3.returned_ref = bf16[32,32,128]{2,1,0:T(8,128)(2,1)S(1)} async-done(((bf16[32,32,128]{2,1,0:T(8,128)(2,1)}), bf16[32,32,128]{2,1,0:T(8,128)(2,1)S(1)}, u32[]{:S(2)}, u32[]{:S(2)}) %all-to-all-start.3) | async-done | bytes 262176 | tf_op jit(solution)/shard_map/all_to_all | solution.py:276
  82.9 0.7 final.1
Async XLA Ops:
  21.7 4.7 %copy-start.4 = (bf16[512,512]{1,0:T(8,128)(2,1)S(1)}, bf16[512,512]{1,0:T(8,128)(2,1)}, u32[]{:S(2)}) copy-start(bf16[512,512]{1,0:T(8,128)(2,1)} %grad_ref.5) | copy-start | bytes 1572868
  23.6 2.8 %copy-start = (bf16[512,128]{1,0:T(8,128)(2,1)S(1)}, bf16[512,128]{1,0:T(8,128)(2,1)}, u32[]{:S(2)}) copy-start(bf16[512,128]{1,0:T(8,128)(2,1)} %keys_ref.3) | copy-start | bytes 393220
  23.6 2.8 %copy-start.1 = (bf16[512,128]{1,0:T(8,128)(2,1)S(1)}, bf16[512,128]{1,0:T(8,128)(2,1)}, u32[]{:S(2)}) copy-start(bf16[512,128]{1,0:T(8,128)(2,1)} %values_ref.3) | copy-start | bytes 393220
  23.6 2.8 %copy-start.2 = (s32[1,2]{1,0:T(1,128)S(1)}, s32[1,2]{1,0:T(1,128)}, u32[]{:S(2)}) copy-start(s32[1,2]{1,0:T(1,128)} %sel_ref.3) | copy-start | bytes 28
  23.6 2.8 %copy-start.3 = (bf16[512,512]{1,0:T(8,128)(2,1)S(1)}, bf16[512,512]{1,0:T(8,128)(2,1)}, u32[]{:S(2)}) copy-start(bf16[512,512]{1,0:T(8,128)(2,1)} %queries_ref.5) | copy-start | bytes 1572868
  23.7 18.4 %all-to-all-start.1 = ((bf16[32,2,32,128]{3,2,1,0:T(8,128)(2,1)}), bf16[32,2,32,128]{3,2,1,0:T(8,128)(2,1)S(1)}, u32[]{:S(2)}, u32[]{:S(2)}) async-start(bf16[32,2,32,128]{3,2,1,0:T(8,128)(2,1)} %get-tuple-element.20), calls=%async_computation.1 | async-start | bytes 1048576 | tf_op jit(solution)/shard_map/all_to_all | solution.py:276
  69.3 13.6 %all-to-all-start.3 = ((bf16[32,32,128]{2,1,0:T(8,128)(2,1)}), bf16[32,32,128]{2,1,0:T(8,128)(2,1)S(1)}, u32[]{:S(2)}, u32[]{:S(2)}) async-start(bf16[32,32,128]{2,1,0:T(8,128)(2,1)} %sum.1), calls=%async_computation.3 | async-start | bytes 524288 | tf_op jit(solution)/shard_map/all_to_all | solution.py:276
